TPU v7x, 32 devices: a whole 2x2x4 slice. The times are simulated.
32 devices in a mesh: rep: 1, dp: 32 (over x, y, z, core).
Axes of the slice: x: 2, y: 2, z: 4, core: 2. Of those that a mesh axis runs over, the one named last changes fastest.
Arguments:
- x: bfloat16 [32, 2048, 1024], P(('rep', 'dp'))
- dy: bfloat16 [32, 2048, 1024], P(('rep', 'dp'))
- w_gate: bfloat16 [2, 1024, 4096], P(None, 'dp')
- w_up: bfloat16 [2, 1024, 4096], P(None, 'dp')
- w_down: bfloat16 [2, 4096, 1024], P(None, 'dp')
Outputs:
- output 1: bfloat16 [32, 2048, 1024], P(('rep', 'dp'))
- output 2: bfloat16 [2, 1024, 4096], P('rep', 'dp')
- output 3: bfloat16 [2, 1024, 4096], P('rep', 'dp')
- output 4: bfloat16 [2, 4096, 1024], P('rep', 'dp')
All inputs are finite; a program needn't handle non-finite values.
Results may differ from a plain program's by a relative error of at most 0.018.
Values are sent between devices in bfloat16 or wider.
A program may use at most 2 GiB of HBM per device.

v0:
```python
import jax
import jax.numpy as jnp
from jax import lax

NAMES = ("w_gate", "w_up", "w_down")


def matmul(a, w):
    return jnp.dot(a, w, preferred_element_type=jnp.float32).astype(jnp.bfloat16)


def normed(h):
    wide = h.astype(jnp.float32)
    scale = lax.rsqrt(jnp.mean(wide**2, -1, keepdims=True) + 1e-6)
    return (wide * scale).astype(jnp.bfloat16)


def layer(h, w):
    a = normed(h)
    gate = jnp.dot(a, w["w_gate"], preferred_element_type=jnp.float32)
    up = jnp.dot(a, w["w_up"], preferred_element_type=jnp.float32)
    return h + matmul((jax.nn.silu(gate) * up).astype(jnp.bfloat16), w["w_down"])


def stack(weights, h):
    for number in range(weights["w_gate"].shape[0]):
        h = layer(h, {name: w[number] for name, w in weights.items()})
    return h


def solution(mesh):
    groups = mesh.shape["rep"]

    def step(x, dy, *weights):
        shape = x.shape
        x, dy = (t.reshape(groups, -1, *t.shape[1:]) for t in (x, dy))

        def of_a_group(x, dy):
            _, back = jax.vjp(stack, dict(zip(NAMES, weights, strict=True)), x)
            by_weights, by_x = back(dy)
            return (by_x, *(by_weights[name] for name in NAMES))

        by_x, *by_weights = jax.vmap(of_a_group)(x, dy)
        return (by_x.reshape(shape), *(t.reshape(-1, *t.shape[2:]) for t in by_weights))

    return step
```

profile of v0, /device:TPU:0, one launch (start us, length us, event | category | flops | bytes accessed | tf_op | source)
XLA Modules:
  0.0 2509.9 jit_solution(17941799247112262861)
XLA Ops:
  43.0 267.9 %while.13 = (bf16[1,2048,1024]{2,1,0:T(8,128)(2,1)}, bf16[1,128,1024]{2,1,0:T(8,128)(2,1)S(1)}, bf16[1,2048,4096]{1,2,0:T(8,128)(2,1)}, bf16[1,128,1024]{2,1,0:T...) while((bf16[1,2048,1024]{2,1,0:T(8,128)(2,1)}, ...), condition=%wide.windowed_dot_general_cond_ag, body=%wide.windowed_dot_general_body_ag.sunk | while | flops 2148007936 | bytes 19923484 | solution.py:9
  69.2 11.2 collective-permute-done.1
  138.1 10.6 collective-permute-done.1
  232.5 10.8 collective-permute-done.1
  310.9 20.9 copy.2
  331.7 25.4 %fusion.204 = f32[2048,4096]{1,0:T(8,128)} fusion(bf16[1,1024,4096]{2,1,0:T(8,128)(2,1)} %all-gather.27.cloned.1.call-done, bf16[1,2048,1024]{1,2,0:T(8,128)(2,1)} %fusion.187), kind=kOutput, calls=%fused_computation.257 | convolution fusion | flops 17179869184 | bytes 46137344 | tf_op jit(solution)/vmap(jvp())/dot_general | solution.py:20
  357.1 39.0 %fusion.176 = (bf16[1,2048,4096]{2,1,0:T(8,128)(2,1)}, f32[2048,4096]{1,0:T(8,128)}) fusion(f32[2048,4096]{1,0:T(8,128)} %fusion.204, bf16[1,1024,4096]{2,1,0:T(8,128)(2,1)} %all-gather.29.cloned.1.call-done, bf16[1,2048,1024]{1,2,0:T(8,128)(2,1)} %fusion.187), kind=kOutput, calls=%fused_computation.215 | convolution fusion | flops 17230200832 | bytes 96468992 | tf_op jit(solution)/vmap(jvp())/dot_general | solution.py:21
  396.1 22.6 copy.6
  418.6 23.6 fusion.189
  447.3 25.6 %fusion.196 = f32[2048,4096]{1,0:T(8,128)} fusion(bf16[1,1024,4096]{2,1,0:T(8,128)(2,1)} %all-gather.33.cloned.1.call-done, bf16[1,2048,1024]{1,2,0:T(8,128)(2,1)} %fusion.190), kind=kOutput, calls=%fused_computation.249 | convolution fusion | flops 17179869184 | bytes 46137344 | tf_op jit(solution)/vmap(jvp())/dot_general | solution.py:20
  473.0 38.5 %fusion.170 = (bf16[1,2048,4096]{2,1,0:T(8,128)(2,1)}, f32[2048,4096]{1,0:T(8,128)}) fusion(f32[2048,4096]{1,0:T(8,128)} %fusion.196, bf16[1,1024,4096]{2,1,0:T(8,128)(2,1)} %all-gather.35.cloned.1.call-done, bf16[1,2048,1024]{1,2,0:T(8,128)(2,1)} %fusion.190), kind=kOutput, calls=%fused_computation.205 | convolution fusion | flops 17230200832 | bytes 96468992 | tf_op jit(solution)/vmap(jvp())/dot_general | solution.py:21
  511.4 22.7 copy.4
  534.1 297.1 %while.18 = (bf16[1,2048,4096]{1,2,0:T(8,128)(2,1)}, bf16[1,2048,1024]{2,1,0:T(8,128)(2,1)}, f32[128,1024]{1,0:T(8,128)S(1)}, f32[128,1024]{1,0:T(8,128)}, u32[]...) while((bf16[1,2048,4096]{1,2,0:T(8,128)(2,1)}, ...), condition=%wide.windowed_dot_general_cond_rs.4.clone, body=%wide.windowed_dot_general_body_rs.4.clone.sunk | while | flops 2152464384 | bytes 60818000 | solution.py:9
  831.2 34.2 %convert_multiply_fusion.3 = (bf16[1,2048,4096]{2,1,0:T(8,128)(2,1)}, bf16[1,2048,4096]{2,1,0:T(8,128)(2,1)S(1)}) fusion(f32[2048,4096]{1,0:T(8,128)} %fusion.196, bf16[1,2048,4096]{2,1,0:T(8,128)(2,1)} %copy.2, f32[2048,4096]{1,0:T(8,128)} %get-tuple-element.290), kind=kLoop, calls=%fused_computation.193 | loop fusion | flops 125829120 | bytes 117440512 | tf_op jit(solution)/vmap(transpose(jvp()))/mul | solution.py:22
  865.5 23.7 fusion.168
  889.2 25.1 %fusion.191 = (f32[2048]{0:T(1024)S(1)}, bf16[2048,1024]{0,1:T(8,128)(2,1)S(1)}) fusion(bf16[1,2048,1024]{1,2,0:T(8,128)(2,1)S(1)} %copy-done.20, bf16[2048,1024]{0,1:T(8,128)(2,1)} %fusion.168, bf16[1,1024,4096]{2,1,0:T(8,128)(2,1)} %all-gather.35.cloned.1.call-done, bf16[1,2048,4096]{2,1,0:T(8,128)(2,1)} %get-tuple-element.694), kind=kOutput, calls=%fused_computation.244 | convolution fusion | flops 17190352896 | bytes 37756928 | tf_op jit(solution)/vmap(transpose(jvp()))/dot_general | solution.py:21
  925.7 296.5 %while.19 = (bf16[1,2048,1024]{2,1,0:T(8,128)(2,1)}, bf16[1,2048,4096]{1,2,0:T(8,128)(2,1)}, f32[1024,128]{0,1:T(8,128)S(1)}, f32[1024,128]{0,1:T(8,128)}, u32[]...) while((bf16[1,2048,1024]{2,1,0:T(8,128)(2,1)}, ...), condition=%wide.windowed_dot_general_cond_rs.5.clone, body=%wide.windowed_dot_general_body_rs.5.clone.sunk | while | flops 2152464384 | bytes 60818000 | solution.py:9
  1223.0 284.0 %while.16 = (bf16[1,2048,4096]{2,1,0:T(8,128)(2,1)}, bf16[1,2048,1024]{1,2,0:T(8,128)(2,1)}, f32[4096,32]{0,1:T(8,128)S(1)}, f32[4096,32]{0,1:T(8,128)}, u32[]{:...) while((bf16[1,2048,4096]{2,1,0:T(8,128)(2,1)}, ...), condition=%wide.windowed_dot_general_cond_rs.2.clone, body=%wide.windowed_dot_general_body_rs.2.clone.sunk | while | flops 2149318656 | bytes 60818000 | solution.py:21
  1507.1 46.1 %convert_multiply_fusion.1 = (bf16[1,2048,4096]{2,1,0:T(8,128)(2,1)}, bf16[1,2048,4096]{2,1,0:T(8,128)(2,1)}) fusion(f32[2048,4096]{1,0:T(8,128)} %fusion.204, f32[2048,4096]{1,0:T(8,128)} %get-tuple-element.282, bf16[1,4096,1024]{2,1,0:T(8,128)(2,1)} %all-gather.31.cloned.1.call-done, bf16[1,2048,1024]{1,2,0:T(8,128)(2,1)} %fusion.207), kind=kOutput, calls=%fused_computation.191 | convolution fusion | flops 17314086912 | bytes 113246208 | tf_op jit(solution)/vmap(transpose(jvp()))/dot_general | solution.py:9
  1553.1 288.6 %while.17 = (bf16[1,2048,4096]{2,1,0:T(8,128)(2,1)}, bf16[1,2048,1024]{1,2,0:T(8,128)(2,1)}, f32[4096,32]{0,1:T(8,128)S(1)}, f32[4096,32]{0,1:T(8,128)}, u32[]{:...) while((bf16[1,2048,4096]{2,1,0:T(8,128)(2,1)}, ...), condition=%wide.windowed_dot_general_cond_rs.3.clone, body=%wide.windowed_dot_general_body_rs.3.clone.sunk | while | flops 2149318656 | bytes 60818000 | solution.py:21
  1842.6 307.0 %while.14 = (bf16[1,2048,4096]{2,1,0:T(8,128)(2,1)}, bf16[1,2048,1024]{1,2,0:T(8,128)(2,1)}, f32[4096,32]{0,1:T(8,128)S(1)}, f32[4096,32]{0,1:T(8,128)}, u32[]{:...) while((bf16[1,2048,4096]{2,1,0:T(8,128)(2,1)}, ...), condition=%wide.windowed_dot_general_cond_rs.clone, body=%wide.windowed_dot_general_body_rs.clone.sunk | while | flops 2149318656 | bytes 62915180 | solution.py:20
  2150.4 273.7 %while.15 = (bf16[1,2048,4096]{2,1,0:T(8,128)(2,1)}, bf16[1,2048,1024]{1,2,0:T(8,128)(2,1)}, f32[4096,32]{0,1:T(8,128)S(1)}, f32[4096,32]{0,1:T(8,128)S(1)}, u32...) while((bf16[1,2048,4096]{2,1,0:T(8,128)(2,1)}, ...), condition=%wide.windowed_dot_general_cond_rs.1.clone, body=%wide.windowed_dot_general_body_rs.1.clone.sunk | while | flops 2149318656 | bytes 60818000 | solution.py:20
  2424.9 24.7 fusion.164
  2449.6 21.9 fusion.188
  (939 shorter events, 2065.5 us)
Async XLA Ops:
  7.2 324.6 %all-gather.27.cloned.1.call-start = ((), (), s32[]{:S(2)}) async-start(), calls=%async_computation | async-start | bytes 8650752 | tf_op jit(solution)/vmap(jvp())/squeeze | solution.py:27
  9.1 348.0 %all-gather.29.cloned.1.call-start = ((), (), s32[]{:S(2)}) async-start(), calls=%async_computation.1 | async-start | bytes 8650752 | tf_op jit(solution)/vmap(jvp())/squeeze | solution.py:27
  11.1 407.5 %all-gather.31.cloned.1.call-start = ((), (), s32[]{:S(2)}) async-start(), calls=%async_computation.2 | async-start | bytes 8650752 | tf_op jit(solution)/vmap(jvp())/squeeze | solution.py:27
  12.9 434.4 %all-gather.33.cloned.1.call-start = ((), (), s32[]{:S(2)}) async-start(), calls=%async_computation.3 | async-start | bytes 8650752 | tf_op jit(solution)/vmap(jvp())/squeeze | solution.py:27
  13.5 459.5 %all-gather.35.cloned.1.call-start = ((), (), s32[]{:S(2)}) async-start(), calls=%async_computation.4 | async-start | bytes 8650752 | tf_op jit(solution)/vmap(jvp())/squeeze | solution.py:27
  13.5 23.4 collective-permute-start.28
  588.5 17.8 collective-permute-start.22
  588.5 17.7 collective-permute-start.23
  663.1 17.8 collective-permute-start.22
  737.8 17.8 collective-permute-start.22
  812.4 17.8 collective-permute-start.22
  831.2 1655.3 %collective-permute-start.33 = (f32[128,1024]{1,0:T(8,128)}, f32[128,1024]{1,0:T(8,128)}, u32[]{:S(2)}, u32[]{:S(2)}) collective-permute-start(f32[128,1024]{1,0:T(8,128)} %get-tuple-element.52), channel_id=46, source_target_pairs={{0,1},{1,2},{2,3},{3,4},{4,5},{5,6},{6,7},{7,8},{8,9},{9,10},{10,1... | collective-permute-start | bytes 1572872 | tf_op jit(solution)/vmap(transpose(jvp()))/dot_general | solution.py:9
  979.5 17.8 collective-permute-start.26
  979.6 17.7 collective-permute-start.27
  1054.2 17.8 collective-permute-start.26
  1054.2 17.7 collective-permute-start.27
  1128.8 17.8 collective-permute-start.26
  1203.5 17.8 collective-permute-start.26
  1222.3 1265.4 %collective-permute-start.34 = (f32[1024,128]{0,1:T(8,128)}, f32[1024,128]{0,1:T(8,128)}, u32[]{:S(2)}, u32[]{:S(2)}) collective-permute-start(f32[1024,128]{0,1:T(8,128)} %get-tuple-element.54), channel_id=52, source_target_pairs={{0,1},{1,2},{2,3},{3,4},{4,5},{5,6},{6,7},{7,8},{8,9},{9,10},{10,1... | collective-permute-start | bytes 1572872 | tf_op jit(solution)/vmap(transpose(jvp()))/dot_general | solution.py:9
  1223.1 22.7 collective-permute-start.12
  1223.2 22.6 collective-permute-start.13
  1507.1 977.2 %collective-permute-start.31 = (f32[4096,32]{0,1:T(8,128)}, f32[4096,32]{0,1:T(8,128)}, u32[]{:S(2)}, u32[]{:S(2)}) collective-permute-start(f32[4096,32]{0,1:T(8,128)} %get-tuple-element.48), channel_id=34, source_target_pairs={{0,1},{1,2},{2,3},{3,4},{4,5},{5,6},{6,7},{7,8},{8,9},{9,10},{10,1... | collective-permute-start | bytes 1572872 | tf_op jit(solution)/vmap(transpose(jvp()))/dot_general | solution.py:21
  2424.1 61.3 %collective-permute-start.32 = (f32[4096,32]{0,1:T(8,128)}, f32[4096,32]{0,1:T(8,128)}, u32[]{:S(2)}, u32[]{:S(2)}) collective-permute-start(f32[4096,32]{0,1:T(8,128)} %get-tuple-element.50), channel_id=40, source_target_pairs={{0,1},{1,2},{2,3},{3,4},{4,5},{5,6},{6,7},{7,8},{8,9},{9,10},{10,1... | collective-permute-start | bytes 1572872 | tf_op jit(solution)/vmap(transpose(jvp()))/dot_general | solution.py:21
  2484.3 17.8 collective-permute-start.30
  (256 other events, 5032.7 us)
Sparse Core Ops, SparseCore 0:
  11.0 90.4 all-gather.26
  104.5 86.4 all-gather.28
  194.0 92.1 all-gather.30
  289.0 81.0 all-gather.32
  373.0 75.9 all-gather.34
where the time goes:
time: 2530 us; the launch traced here: 2510 us
  matrix products  1040 us (41%)
  starting transfers between devices  551 us (22%)
  waiting for transfers between devices  524 us (21%)
  other arithmetic  232 us (9%)
  local copies, waits for them, and re-layouts  143 us (6%)
    dot_general x99, waiting for transfers between devices, matmul(): jnp.dot(a, w, preferred_element_type=jnp.float32).astype(jnp.bfloat16)  417 us
    dot_general x36, matrix products, layer(): up = jnp.dot(a, w['w_up'], preferred_element_type=jnp.float32)  410 us
    dot_general x36, matrix products, layer(): gate = jnp.dot(a, w['w_gate'], preferred_element_type=jnp.float32)  385 us
    dot_general x50, matrix products, matmul(): jnp.dot(a, w, preferred_element_type=jnp.float32).astype(jnp.bfloat16)  245 us
    dot_general x99, starting transfers between devices, matmul(): jnp.dot(a, w, preferred_element_type=jnp.float32).astype(jnp.bfloat16)  206 us
    dot_general x66, starting transfers between devices, layer(): up = jnp.dot(a, w['w_up'], preferred_element_type=jnp.float32)  173 us
    dot_general x66, starting transfers between devices, layer(): gate = jnp.dot(a, w['w_gate'], preferred_element_type=jnp.float32)  172 us
    unnamed x78, local copies, waits for them, and re-layouts  77.5 us
  transfers between devices with their start and end apart: 236, of which 111 were waited for; matrix products, arithmetic and copies ran while one was open for 53% of the time, Pallas kernels for 0%

commit v1 on v0

v1 whole, which is shorter than its diff:
```python
import jax
import jax.numpy as jnp
from jax import lax
from jax.sharding import PartitionSpec as P

BF = jnp.bfloat16
F32 = jnp.float32


def dot(a, b, dims):
    return lax.dot_general(a, b, (dims, ((), ())), preferred_element_type=F32)


NN = ((1,), (0,))
NT = ((1,), (1,))
TN = ((0,), (0,))


def normed(h):
    wide = h.astype(F32)
    scale = lax.rsqrt(jnp.mean(wide**2, -1, keepdims=True) + 1e-6)
    return (wide * scale).astype(BF), scale


def norm_back(h, scale, da):
    wide, da = h.astype(F32), da.astype(F32)
    inner = jnp.mean(da * wide, -1, keepdims=True)
    return scale * da - wide * (scale * scale * scale * inner)


def act_back(gate, up, dhid):
    s = jax.nn.sigmoid(gate)
    silu = gate * s
    return (dhid * up * (s + silu * (1 - s))).astype(BF), (dhid * silu).astype(BF)


def solution(mesh):
    axes = ("rep", "dp")

    def gather(w):
        return lax.all_gather(w, "dp", axis=0, tiled=True)

    def scatter(term):
        return lax.psum_scatter(term, "dp", scatter_dimension=0, tiled=True)

    def step(x, dy, w_gate, w_up, w_down):
        h, dh = x[0], dy[0]
        layers = w_gate.shape[0]
        full = [[gather(w[l]) for w in (w_gate, w_up, w_down)] for l in range(layers)]
        saved = []
        for l in range(layers):
            wg, wu, wd = full[l]
            a, scale = normed(h)
            gate, up = dot(a, wg, NN), dot(a, wu, NN)
            hid = (jax.nn.silu(gate) * up).astype(BF)
            saved.append((h, scale, a, gate, up, hid))
            if l < layers - 1:
                h = h + dot(hid, wd, NN).astype(BF)
        grads = [None] * layers
        for l in reversed(range(layers)):
            wg, wu, wd = full[l]
            h, scale, a, gate, up, hid = saved[l]
            dwd = scatter(dot(hid, dh, TN).astype(BF))
            dhid = dot(dh, wd, NT).astype(BF).astype(F32)
            dgate, dup = act_back(gate, up, dhid)
            dwg = scatter(dot(a, dgate, TN).astype(BF))
            dwu = scatter(dot(a, dup, TN).astype(BF))
            da = dot(dgate, wg, NT).astype(BF) + dot(dup, wu, NT).astype(BF)
            dh = dh + norm_back(h, scale, da).astype(BF)
            grads[l] = (dwg, dwu, dwd)
        return (dh[None], *(jnp.stack(g) for g in zip(*grads)))

    seqs, rows = P(axes, None, None), P(None, "dp", None)
    outs = P("rep", "dp", None)
    return jax.shard_map(
        step, mesh=mesh, in_specs=(seqs, seqs, rows, rows, rows), out_specs=(seqs, outs, outs, outs), check_vma=False
    )
```

time: 2530 us -> 1540 us (0.61)
  starting transfers between devices: 551 us -> 0.49 us
  matrix products: 1040 us -> 492 us
  waiting for transfers between devices: 524 us -> 983 us
  other arithmetic: 232 us -> 18.6 us
  local copies, waits for them, and re-layouts: 143 us -> 28.8 us
    reduce_scatter x0 -> x6, waiting for transfers between devices: none -> 664 us  [scatter(): return lax.psum_scatter(term, 'dp', scatter_dimension=0, tiled=True)]
    dot_general x231 -> x0, starting transfers between devices: 551 us -> none  [the longest x99 206 us: matmul(): jnp.dot(a, w, preferred_element_type=jnp.float32).astype(jnp.bfloat16)]
    dot_general x122 -> x17, matrix products: 1040 us -> 492 us  [dot(): return lax.dot_general(a, b, (dims, ((), ())), preferred_element_type=F32)]
    dot_general x231 -> x0, waiting for transfers between devices: 523 us -> none  [the longest x99 417 us: matmul(): jnp.dot(a, w, preferred_element_type=jnp.float32).astype(jnp.bfloat16)]
    all_gather x0 -> x6, waiting for transfers between devices: none -> 318 us  [gather(): return lax.all_gather(w, 'dp', axis=0, tiled=True)]
    dot_general x192 -> x0, other arithmetic: 168 us -> none
    dot_general x50 -> x0, local copies, waits for them, and re-layouts: 60.3 us -> none  [the longest x34 54 us: matmul(): jnp.dot(a, w, preferred_element_type=jnp.float32).astype(jnp.bfloat16)]
    unnamed x78 -> x29, local copies, waits for them, and re-layouts: 77.5 us -> 23.2 us
  transfers between devices with their start and end apart: 236 -> 12, of which waited for: 111 -> 11; matrix products, arithmetic and copies ran while one was open for 53% -> 26% of each run, Pallas kernels for 0% -> 0%
where the time goes in v1:
time: 1540 us
  waiting for transfers between devices  983 us (64%)
  matrix products  492 us (32%)
  local copies, waits for them, and re-layouts  28.8 us (2%)
  other arithmetic  18.6 us (1%)
    reduce_scatter x6, waiting for transfers between devices, scatter(): return lax.psum_scatter(term, 'dp', scatter_dimension=0, tiled=True)  664 us
    dot_general x17, matrix products, dot(): return lax.dot_general(a, b, (dims, ((), ())), preferred_element_type=F32)  492 us
    all_gather x6, waiting for transfers between devices, gather(): return lax.all_gather(w, 'dp', axis=0, tiled=True)  318 us
  transfers between devices with their start and end apart: 12, of which 11 were waited for; matrix products, arithmetic and copies ran while one was open for 26% of the time, Pallas kernels for 0%

profile of v1, /device:TPU:0, one launch (start us, length us, event | category | flops | bytes accessed | tf_op | source)
XLA Modules:
  0.0 1537.5 jit_solution(17974714811732831486)
XLA Ops:
  31.4 59.9 %all-gather.13.cloned.1.call-done = bf16[1,1024,4096]{2,1,0:T(8,128)(2,1)} async-done(((bf16[1,32,4096]{2,1,0:T(8,128)(2,1)}), bf16[1,1024,4096]{2,1,0:T(8,128)(2,1)}) %all-gather.13.cloned.1.call-update) | async-done | bytes 8388624 | tf_op jit(solution)/shard_map/all_gather | solution.py:41
  91.3 24.4 %fusion.37 = f32[2048,4096]{1,0:T(8,128)} fusion(bf16[1,1024,4096]{2,1,0:T(8,128)(2,1)} %all-gather.13.cloned.1.call-done, bf16[1,2048,1024]{1,2,0:T(8,128)(2,1)} %copy.10, f32[2048]{0:T(1024)S(1)} %add_rsqrt_fusion.1), kind=kOutput, calls=%fused_computation.57 | convolution fusion | flops 17186160640 | bytes 46145536 | tf_op jit(solution)/shard_map/dot_general | solution.py:11
  115.7 54.6 %all-gather.15.cloned.1.call-done = bf16[1,1024,4096]{2,1,0:T(8,128)(2,1)} async-done(((bf16[1,32,4096]{2,1,0:T(8,128)(2,1)}), bf16[1,1024,4096]{2,1,0:T(8,128)(2,1)}) %all-gather.15.cloned.1.call-update) | async-done | bytes 8388624 | tf_op jit(solution)/shard_map/all_gather | solution.py:41
  170.3 39.1 %multiply_convert_fusion.1 = (bf16[2048,4096]{1,0:T(8,128)(2,1)}, f32[2048,4096]{1,0:T(8,128)}) fusion(f32[2048,4096]{1,0:T(8,128)} %fusion.37, bf16[1,1024,4096]{2,1,0:T(8,128)(2,1)} %all-gather.15.cloned.1.call-done, bf16[1,2048,1024]{1,2,0:T(8,128)(2,1)} %copy.10, f32[2048]{0:T(1024)S(1)} %add_rsqrt_fusion.1), kind=kOutput, calls=%fused_computation.12 | convolution fusion | flops 17236492288 | bytes 96477184 | tf_op jit(solution)/shard_map/dot_general | solution.py:11
  209.4 39.9 %all-gather.17.cloned.1.call-done = bf16[1,4096,1024]{2,1,0:T(8,128)(2,1)} async-done(((bf16[1,128,1024]{2,1,0:T(8,128)(2,1)}), bf16[1,4096,1024]{2,1,0:T(8,128)(2,1)}) %all-gather.17.cloned.1.call-update) | async-done | bytes 8388624 | tf_op jit(solution)/shard_map/all_gather | solution.py:41
  249.3 24.6 %fusion.16 = (f32[2048]{0:T(1024)S(1)}, bf16[2048,1024]{0,1:T(8,128)(2,1)}) fusion(bf16[2048,4096]{1,0:T(8,128)(2,1)} %get-tuple-element.14, bf16[1,4096,1024]{2,1,0:T(8,128)(2,1)} %all-gather.17.cloned.1.call-done, bf16[1,2048,1024]{1,2,0:T(8,128)(2,1)} %copy.10), kind=kOutput, calls=%fused_computation.36 | convolution fusion | flops 17190352896 | bytes 33562624 | tf_op jit(solution)/shard_map/dot_general | solution.py:11
  274.5 54.3 %all-gather.23.cloned.1.call-done = bf16[1,1024,4096]{2,1,0:T(8,128)(2,1)} async-done(((bf16[1,32,4096]{2,1,0:T(8,128)(2,1)}), bf16[1,1024,4096]{2,1,0:T(8,128)(2,1)}) %all-gather.23.cloned.1.call-update) | async-done | bytes 8388624 | tf_op jit(solution)/shard_map/all_gather | solution.py:41
  328.8 24.8 %fusion.21 = f32[2048,4096]{1,0:T(8,128)} fusion(bf16[1,1024,4096]{2,1,0:T(8,128)(2,1)} %all-gather.23.cloned.1.call-done, bf16[2048,1024]{0,1:T(8,128)(2,1)} %get-tuple-element.17, f32[2048]{0:T(1024)S(1)} %add_rsqrt_fusion), kind=kOutput, calls=%fused_computation.41 | convolution fusion | flops 17186160640 | bytes 46145536 | tf_op jit(solution)/shard_map/dot_general | solution.py:11
  353.6 54.0 %all-gather.19.cloned.1.call-done = bf16[1,4096,1024]{2,1,0:T(8,128)(2,1)} async-done(((bf16[1,128,1024]{2,1,0:T(8,128)(2,1)}), bf16[1,4096,1024]{2,1,0:T(8,128)(2,1)}) %all-gather.19.cloned.1.call-update) | async-done | bytes 8388624 | tf_op jit(solution)/shard_map/all_gather | solution.py:41
  407.6 24.3 %convolution_convert_fusion.1 = bf16[2048,4096]{1,0:T(8,128)(2,1)} fusion(bf16[1,4096,1024]{2,1,0:T(8,128)(2,1)} %all-gather.19.cloned.1.call-done, bf16[1,2048,1024]{2,1,0:T(8,128)(2,1)} %param.6), kind=kOutput, calls=%fused_computation.18 | convolution fusion | flops 17188257792 | bytes 29360128 | tf_op jit(solution)/shard_map/dot_general | solution.py:11
  431.9 55.1 %all-gather.21.cloned.1.call-done = bf16[1,1024,4096]{2,1,0:T(8,128)(2,1)} async-done(((bf16[1,32,4096]{2,1,0:T(8,128)(2,1)}), bf16[1,1024,4096]{2,1,0:T(8,128)(2,1)}) %all-gather.21.cloned.1.call-update) | async-done | bytes 8388624 | tf_op jit(solution)/shard_map/all_gather | solution.py:41
  487.0 46.7 %fusion.1 = (bf16[2048,4096]{1,0:T(8,128)(2,1)}, f32[2048,4096]{1,0:T(8,128)}) fusion(bf16[2048,4096]{1,0:T(8,128)(2,1)} %convolution_convert_fusion.1, f32[2048,4096]{1,0:T(8,128)} %fusion.21, bf16[1,1024,4096]{2,1,0:T(8,128)(2,1)} %all-gather.21.cloned.1.call-done, bf16[2048,1024]{0,1:T(8,128)(2,1)} %get-tuple-element.17, f32[2048]{0:T(1024)S(1)} %add_rsqrt_fusion), kind=kOutput, calls=%fused_computation.5 | convolution fusion | flops 17278435328 | bytes 113254400 | tf_op jit(solution)/shard_map/dot_general | solution.py:11
  557.5 32.4 %fusion.18 = (f32[2048]{0:T(1024)S(1)}, bf16[2048,1024]{0,1:T(8,128)(2,1)}) fusion(bf16[2048,1024]{0,1:T(8,128)(2,1)} %get-tuple-element.17, bf16[2048,1024]{0,1:T(8,128)(2,1)} %fusion.19, bf16[1,1024,4096]{2,1,0:T(8,128)(2,1)} %all-gather.21.cloned.1.call-done, bf16[2048,4096]{1,0:T(8,128)(2,1)} %convolution_convert_fusion.1, f32[2048,4096]{1,0:T(8,128)} %fusion.21), kind=kOutput, calls=%fused_computation.38 | convolution fusion | flops 17251170304 | bytes 71311360 | tf_op jit(solution)/shard_map/dot_general | solution.py:11
  620.8 30.6 %fusion.39 = bf16[4096,1024]{1,0:T(8,128)(2,1)} fusion(f32[2048,4096]{1,0:T(8,128)} %get-tuple-element.19, bf16[1,2048,1024]{2,1,0:T(8,128)(2,1)} %param.6, f32[2048,4096]{1,0:T(8,128)} %fusion.21), kind=kOutput, calls=%fused_computation.59 | convolution fusion | flops 17234395136 | bytes 79691776 | tf_op jit(solution)/shard_map/dot_general | solution.py:11
  651.4 46.9 %fusion.4 = (bf16[2048,4096]{1,0:T(8,128)(2,1)}, bf16[2048,4096]{1,0:T(8,128)(2,1)}) fusion(f32[2048,4096]{1,0:T(8,128)} %get-tuple-element.15, f32[2048,4096]{1,0:T(8,128)} %fusion.37, bf16[2048,1024]{0,1:T(8,128)(2,1)} %copy-done.2, bf16[1,4096,1024]{2,1,0:T(8,128)(2,1)} %all-gather.17.cloned.1.call-done), kind=kOutput, calls=%fused_computation.8 | convolution fusion | flops 17280532480 | bytes 113246208 | tf_op jit(solution)/shard_map/dot_general | solution.py:11
  698.4 25.6 %convolution_convert_fusion.4 = bf16[1024,4096]{1,0:T(8,128)(2,1)} fusion(bf16[1,2048,1024]{1,2,0:T(8,128)(2,1)S(1)} %copy-done, f32[2048]{0:T(1024)S(1)} %copy-done.8, bf16[2048,4096]{1,0:T(8,128)(2,1)} %get-tuple-element.23, f32[2048,4096]{1,0:T(8,128)} %fusion.37), kind=kOutput, calls=%fused_computation.62 | convolution fusion | flops 17249075200 | bytes 62922752 | tf_op jit(solution)/shard_map/dot_general | solution.py:11
  724.7 27.0 %convolution_convert_fusion.3 = bf16[1024,4096]{1,0:T(8,128)(2,1)} fusion(bf16[2048,1024]{0,1:T(8,128)(2,1)} %get-tuple-element.17, f32[2048]{0:T(1024)S(1)} %copy-done.10, bf16[2048,4096]{1,0:T(8,128)(2,1)} %convolution_convert_fusion.1, f32[2048,4096]{1,0:T(8,128)} %fusion.21), kind=kOutput, calls=%fused_computation.61 | convolution fusion | flops 17249075200 | bytes 62922752 | tf_op jit(solution)/shard_map/dot_general | solution.py:11
  798.0 27.1 %fusion.31 = bf16[2048,1024]{0,1:T(8,128)(2,1)} fusion(bf16[1,1024,4096]{2,1,0:T(8,128)(2,1)} %all-gather.15.cloned.1.call-done, bf16[2048,4096]{1,0:T(8,128)(2,1)} %get-tuple-element.23, f32[2048,4096]{1,0:T(8,128)} %fusion.37), kind=kOutput, calls=%fused_computation.51 | convolution fusion | flops 17238589440 | bytes 62914560 | tf_op jit(solution)/shard_map/dot_general | solution.py:11
  825.1 25.1 %fusion.15 = (f32[2048]{0:T(1024)S(1)}, bf16[2048,1024]{0,1:T(8,128)(2,1)S(1)}) fusion(bf16[1,2048,1024]{1,2,0:T(8,128)(2,1)S(1)} %copy-done.1, bf16[2048,1024]{0,1:T(8,128)(2,1)} %fusion.31, bf16[2048,4096]{1,0:T(8,128)(2,1)} %get-tuple-element.22, bf16[1,1024,4096]{2,1,0:T(8,128)(2,1)} %all-gather.13.cloned.1.call-done), kind=kOutput, calls=%fused_computation.35 | convolution fusion | flops 17192450048 | bytes 37756928 | tf_op jit(solution)/shard_map/dot_general | solution.py:11
  861.1 61.5 %reduce-scatter.17.cloned.1.call-done = bf16[128,1024]{1,0:T(8,128)(2,1)} async-done(((bf16[4096,1024]{1,0:T(8,128)(2,1)}), bf16[128,1024]{1,0:T(8,128)(2,1)}) %reduce-scatter.17.cloned.1.call-update) | async-done | bytes 262160 | tf_op jit(solution)/shard_map/reduce_scatter | solution.py:44
  924.5 149.6 %reduce-scatter.11.cloned.1.call-done = bf16[32,4096]{1,0:T(8,128)(2,1)} async-done(((bf16[1024,4096]{1,0:T(8,128)(2,1)}), bf16[32,4096]{1,0:T(8,128)(2,1)}) %reduce-scatter.11.cloned.1.call-update) | async-done | bytes 262160 | tf_op jit(solution)/shard_map/reduce_scatter | solution.py:44
  1074.2 151.4 %reduce-scatter.13.cloned.1.call-done = bf16[32,4096]{1,0:T(8,128)(2,1)} async-done(((bf16[1024,4096]{1,0:T(8,128)(2,1)}), bf16[32,4096]{1,0:T(8,128)(2,1)}) %reduce-scatter.13.cloned.1.call-update) | async-done | bytes 262160 | tf_op jit(solution)/shard_map/reduce_scatter | solution.py:44
  1227.4 149.7 %reduce-scatter.9.cloned.1.call-done = bf16[32,4096]{1,0:T(8,128)(2,1)} async-done(((bf16[1024,4096]{1,0:T(8,128)(2,1)}), bf16[32,4096]{1,0:T(8,128)(2,1)}) %reduce-scatter.9.cloned.1.call-update) | async-done | bytes 262160 | tf_op jit(solution)/shard_map/reduce_scatter | solution.py:44
  1377.1 151.3 %reduce-scatter.7.cloned.1.call-done = bf16[32,4096]{1,0:T(8,128)(2,1)} async-done(((bf16[1024,4096]{1,0:T(8,128)(2,1)}), bf16[32,4096]{1,0:T(8,128)(2,1)}) %reduce-scatter.7.cloned.1.call-update) | async-done | bytes 262160 | tf_op jit(solution)/shard_map/reduce_scatter | solution.py:44
  (71 shorter events, 142.9 us)
Async XLA Ops:
  7.2 84.1 %all-gather.13.cloned.1.call-start = ((), (), s32[]{:S(2)}) async-start(), calls=%async_computation.12 | async-start | bytes 8650752 | tf_op jit(solution)/shard_map/all_gather | solution.py:41
  9.1 161.2 %all-gather.15.cloned.1.call-start = ((), (), s32[]{:S(2)}) async-start(), calls=%async_computation.13 | async-start | bytes 8650752 | tf_op jit(solution)/shard_map/all_gather | solution.py:41
  11.0 238.3 %all-gather.17.cloned.1.call-start = ((), (), s32[]{:S(2)}) async-start(), calls=%async_computation.14 | async-start | bytes 8650752 | tf_op jit(solution)/shard_map/all_gather | solution.py:41
  13.0 315.8 %all-gather.23.cloned.1.call-start = ((), (), s32[]{:S(2)}) async-start(), calls=%async_computation.17 | async-start | bytes 8650752 | tf_op jit(solution)/shard_map/all_gather | solution.py:41
  13.6 394.0 %all-gather.19.cloned.1.call-start = ((), (), s32[]{:S(2)}) async-start(), calls=%async_computation.15 | async-start | bytes 8650752 | tf_op jit(solution)/shard_map/all_gather | solution.py:41
  14.2 472.9 %all-gather.21.cloned.1.call-start = ((), (), s32[]{:S(2)}) async-start(), calls=%async_computation.16 | async-start | bytes 8650752 | tf_op jit(solution)/shard_map/all_gather | solution.py:41
  14.7 846.4 %reduce-scatter.15.cloned.1.call-start = ((), (), s32[]{:S(2)}) async-start(), calls=%async_computation.10 | async-start | bytes 8650752 | tf_op jit(solution)/shard_map/reduce_scatter | solution.py:44
  24.9 145.4 %copy-start.7 = (f32[2048]{0:T(1024)}, f32[2048]{0:T(1024)S(1)}, u32[]{:S(2)}) copy-start(f32[2048]{0:T(1024)S(1)} %add_rsqrt_fusion.1) | copy-start | bytes 24580
  273.9 0.6 copy-start.11
  274.5 315.5 %copy-start.9 = (f32[2048]{0:T(1024)}, f32[2048]{0:T(1024)S(1)}, u32[]{:S(2)}) copy-start(f32[2048]{0:T(1024)S(1)} %add_rsqrt_fusion) | copy-start | bytes 24580
  557.5 32.4 %copy-start.12 = (f32[2048]{0:T(1024)S(1)}, f32[2048]{0:T(1024)}, u32[]{:S(2)}) copy-start(f32[2048]{0:T(1024)} %copy-done.11) | copy-start | bytes 24580
  557.5 32.5 %copy-start.4 = (bf16[1,2048,1024]{1,2,0:T(8,128)(2,1)S(1)}, bf16[1,2048,1024]{1,2,0:T(8,128)(2,1)}, u32[]{:S(2)}) copy-start(bf16[1,2048,1024]{1,2,0:T(8,128)(2,1)} %copy.9) | copy-start | bytes 12582916
  595.3 2.0 copy-start.2
  620.7 301.9 %reduce-scatter.17.cloned.1.call-start = ((), (), s32[]{:S(2)}) async-start(), calls=%async_computation.11 | async-start | bytes 8650752 | tf_op jit(solution)/shard_map/reduce_scatter | solution.py:44
  651.4 422.8 %reduce-scatter.11.cloned.1.call-start = ((), (), s32[]{:S(2)}) async-start(), calls=%async_computation.8 | async-start | bytes 8650752 | tf_op jit(solution)/shard_map/reduce_scatter | solution.py:44
  651.4 46.9 %copy-start = (bf16[1,2048,1024]{1,2,0:T(8,128)(2,1)S(1)}, bf16[1,2048,1024]{1,2,0:T(8,128)(2,1)}, u32[]{:S(2)}) copy-start(bf16[1,2048,1024]{1,2,0:T(8,128)(2,1)} %copy.10) | copy-start | bytes 12582916
  651.4 46.9 %copy-start.8 = (f32[2048]{0:T(1024)S(1)}, f32[2048]{0:T(1024)}, u32[]{:S(2)}) copy-start(f32[2048]{0:T(1024)} %copy-done.7) | copy-start | bytes 24580
  724.0 0.7 copy-start.10
  724.0 501.5 %reduce-scatter.13.cloned.1.call-start = ((), (), s32[]{:S(2)}) async-start(), calls=%async_computation.9 | async-start | bytes 8650752 | tf_op jit(solution)/shard_map/reduce_scatter | solution.py:44
  751.7 625.4 %reduce-scatter.9.cloned.1.call-start = ((), (), s32[]{:S(2)}) async-start(), calls=%async_computation.7 | async-start | bytes 8650752 | tf_op jit(solution)/shard_map/reduce_scatter | solution.py:44
  774.7 753.7 %reduce-scatter.7.cloned.1.call-start = ((), (), s32[]{:S(2)}) async-start(), calls=%async_computation.6 | async-start | bytes 8650752 | tf_op jit(solution)/shard_map/reduce_scatter | solution.py:44
  797.9 27.1 %copy-start.1 = (bf16[1,2048,1024]{1,2,0:T(8,128)(2,1)S(1)}, bf16[1,2048,1024]{1,2,0:T(8,128)(2,1)}, u32[]{:S(2)}) copy-start(bf16[1,2048,1024]{1,2,0:T(8,128)(2,1)} %copy.10) | copy-start | bytes 12582916
  825.1 25.1 %copy-start.6 = (f32[2048]{0:T(1024)S(1)}, f32[2048]{0:T(1024)}, u32[]{:S(2)}) copy-start(f32[2048]{0:T(1024)} %copy-done.5) | copy-start | bytes 24580
  825.1 25.1 %copy-start.3 = (bf16[2048,1024]{0,1:T(8,128)(2,1)S(1)}, bf16[2048,1024]{0,1:T(8,128)(2,1)}, u32[]{:S(2)}) copy-start(bf16[2048,1024]{0,1:T(8,128)(2,1)} %copy-done.2) | copy-start | bytes 12582916
  (1 other events, 0.6 us)
Sparse Core Ops, SparseCore 0:
  11.5 79.6 all-gather.12
  94.3 75.9 all-gather.14
  173.3 75.9 all-gather.16
  252.7 75.9 all-gather.22
  331.6 75.9 all-gather.18
  411.0 75.9 all-gather.20
  620.9 150.3 reduce-scatter.14
  773.5 149.1 reduce-scatter.16
  925.0 149.1 reduce-scatter.10
  1076.3 149.1 reduce-scatter.12
  1227.8 149.1 reduce-scatter.8
  1379.2 149.1 reduce-scatter.6
